TPU v7x, 32 devices: a whole 2x2x4 slice. The times are simulated.
32 devices in a mesh: gz: 8 (over z, y), gy: 4 (over x, core).
Axes of the slice: x: 2, y: 2, z: 4, core: 2. Of those that a mesh axis runs over, the one named last changes fastest.
Arguments:
- density: float32 [64, 123904], P('gz', 'gy'), may hold values from -6 to 6
Outputs:
- potential: float32 [64, 123904], P('gz', 'gy')
All inputs are finite; a program needn't handle non-finite values.
Results may differ from a plain program's by a relative error of at most 0.00014.
Values sent between devices are 32-bit elements; how exact they have to be, the bound alone decides.
A program may use at most 128 MiB of HBM per device.

v0:
```python
import math

import jax
import jax.numpy as jnp
from jax import lax
from jax.sharding import PartitionSpec as P

NX = 352
NY = 352
SCREEN = 128


HIGHEST = lax.Precision.HIGHEST
TWO_PI = 2.0 * math.pi


def tables(length):
    index = jnp.arange(length, dtype=jnp.int32)
    phase = index[:, None] * index[None, :] % length
    angle = phase.astype(jnp.float32) * (TWO_PI / length)
    return (jnp.cos(angle), jnp.sin(angle), jnp.ones((length, 1), jnp.float32))


def half_tables(length):
    index = jnp.arange(length, dtype=jnp.int32)
    bins = jnp.arange(length // 2, dtype=jnp.int32)
    phase = bins[:, None] * index[None, :] % length
    angle = phase.astype(jnp.float32) * (TWO_PI / length)
    alternate = jnp.where(index % 2 == 0, 1.0, -1.0).astype(jnp.float32)
    sine = jnp.where(bins[:, None] == 0, -alternate[None, :], jnp.sin(angle))
    weight = jnp.where(bins == 0, 1.0, 2.0).astype(jnp.float32)[:, None]
    return (jnp.cos(angle), sine, weight)


def mirror(values):
    return jnp.roll(jnp.flip(values, -1), 1, -1)


def wavenumber(index, length):
    folded = jnp.minimum(index, length - index).astype(jnp.float32)
    return folded * (TWO_PI / length)


def local_part(real_part, imag_part, kappa):
    planes = real_part.shape[0]
    offset = jnp.arange(planes, dtype=jnp.int32)
    distance = jnp.abs(offset[:, None] - offset[None, :]).astype(jnp.float32)

    def per_row(item):
        row_real, row_imag, kappa_row = item
        kernel = jnp.exp(-distance[:, :, None] * kappa_row[None, None, :])
        return (
            jnp.einsum("ijn,jn->in", kernel, row_real, precision=HIGHEST),
            jnp.einsum("ijn,jn->in", kernel, row_imag, precision=HIGHEST),
        )

    out_real, out_imag = lax.map(
        per_row, (jnp.moveaxis(real_part, 1, 0), jnp.moveaxis(imag_part, 1, 0), kappa)
    )
    return (jnp.moveaxis(out_real, 0, 1), jnp.moveaxis(out_imag, 0, 1))


def edge_weights(kappa, planes):
    offset = jnp.arange(planes, dtype=jnp.int32).astype(jnp.float32)[:, None, None]
    w_first = jnp.exp(-offset * kappa[None])
    w_last = jnp.exp(-(planes - 1.0 - offset) * kappa[None])
    return (w_first, w_last)


def edge_sums(real_part, imag_part, w_first, w_last):
    return (
        jnp.sum(w_last * real_part, 0),
        jnp.sum(w_last * imag_part, 0),
        jnp.sum(w_first * real_part, 0),
        jnp.sum(w_first * imag_part, 0),
    )


def far_weights(gap, kappa, planes):
    steps = jnp.maximum(gap, 0).astype(jnp.float32)
    shape = gap.shape + (1,) * kappa.ndim
    weight = jnp.exp(-planes * steps.reshape(shape) * kappa)
    return jnp.where(gap.reshape(shape) >= 0, weight, 0.0)


def assemble(local, carried, kappa, w_first, w_last):
    step = jnp.exp(-kappa)
    lower = w_first * step
    upper = w_last * step
    scale = 0.5 / kappa
    phi_real = (local[0] + lower * carried[0] + upper * carried[2]) * scale
    phi_imag = (local[1] + lower * carried[1] + upper * carried[3]) * scale
    return (phi_real, phi_imag)


def on_device(density):
    planes = density.shape[0]
    width_x = NX
    width_y = NY
    groups_y = lax.axis_size("gy")
    rows_y = width_y // groups_y
    field = density.reshape(planes, rows_y, width_x)
    cos_x, sin_x, weight_x = half_tables(width_x)
    block_x = cos_x.shape[0] // groups_y
    cos_y, sin_y, unused = tables(width_y)
    trans_real = jnp.einsum("kx,zyx->zyk", cos_x, field, precision=HIGHEST)
    trans_imag = -jnp.einsum("kx,zyx->zyk", sin_x, field, precision=HIGHEST)
    trans_real, trans_imag = (
        lax.all_to_all(trans_real, "gy", split_axis=2, concat_axis=1, tiled=True),
        lax.all_to_all(trans_imag, "gy", split_axis=2, concat_axis=1, tiled=True),
    )
    hat_real = jnp.einsum("zyx,yk->zxk", trans_real, cos_y, precision=HIGHEST) + jnp.einsum(
        "zyx,yk->zxk", trans_imag, sin_y, precision=HIGHEST
    )
    hat_imag = jnp.einsum("zyx,yk->zxk", trans_imag, cos_y, precision=HIGHEST) - jnp.einsum(
        "zyx,yk->zxk", trans_real, sin_y, precision=HIGHEST
    )
    index_x = lax.axis_index("gy") * block_x + jnp.arange(block_x, dtype=jnp.int32)
    first = lax.axis_index("gy") == 0
    packed_real = hat_real[:, 0]
    packed_imag = hat_imag[:, 0]
    mirror_real = mirror(packed_real)
    mirror_imag = mirror(packed_imag)
    zero_real = jnp.where(first, 0.5 * (packed_real + mirror_real), packed_real)
    zero_imag = jnp.where(first, 0.5 * (packed_imag - mirror_imag), packed_imag)
    nyquist_real = jnp.where(first, 0.5 * (packed_imag + mirror_imag), 0.0)
    nyquist_imag = jnp.where(first, 0.5 * (mirror_real - packed_real), 0.0)
    hat_real = jnp.concatenate([zero_real[:, None], hat_real[:, 1:], nyquist_real[:, None]], 1)
    hat_imag = jnp.concatenate([zero_imag[:, None], hat_imag[:, 1:], nyquist_imag[:, None]], 1)
    index_x = jnp.concatenate([index_x, jnp.full((1,), width_x // 2, jnp.int32)])
    columns = hat_real.shape[1]
    wave_x = wavenumber(index_x, width_x)
    wave_y = wavenumber(jnp.arange(width_y, dtype=jnp.int32), width_y)
    kappa = jnp.sqrt(1.0 / (SCREEN * SCREEN) + wave_x[:, None] ** 2 + wave_y[None, :] ** 2)
    groups_z = lax.axis_size("gz")
    narrow = width_y // groups_z
    slab_real, slab_imag = (
        lax.all_to_all(hat_real, "gz", split_axis=2, concat_axis=0, tiled=True),
        lax.all_to_all(hat_imag, "gz", split_axis=2, concat_axis=0, tiled=True),
    )
    kappa_sub = lax.dynamic_slice_in_dim(kappa, lax.axis_index("gz") * narrow, narrow, 1)
    seg_real = slab_real.reshape(groups_z, planes, columns, narrow)
    seg_imag = slab_imag.reshape(groups_z, planes, columns, narrow)
    w_first, w_last = edge_weights(kappa_sub, planes)
    local = jax.vmap(lambda one_real, one_imag: local_part(one_real, one_imag, kappa_sub))(
        seg_real, seg_imag
    )
    edges = jax.vmap(lambda one_real, one_imag: edge_sums(one_real, one_imag, w_first, w_last))(
        seg_real, seg_imag
    )
    segment = jnp.arange(groups_z, dtype=jnp.int32)
    w_up = far_weights(segment[:, None] - 1 - segment[None, :], kappa_sub, planes)
    w_down = far_weights(segment[None, :] - segment[:, None] - 1, kappa_sub, planes)
    carried = (
        jnp.einsum("srmn,rmn->smn", w_up, edges[0], precision=HIGHEST),
        jnp.einsum("srmn,rmn->smn", w_up, edges[1], precision=HIGHEST),
        jnp.einsum("srmn,rmn->smn", w_down, edges[2], precision=HIGHEST),
        jnp.einsum("srmn,rmn->smn", w_down, edges[3], precision=HIGHEST),
    )
    carried = tuple((value[:, None] for value in carried))
    phi_real, phi_imag = assemble(local, carried, kappa_sub, w_first[None], w_last[None])
    phi_real = phi_real.reshape(groups_z * planes, columns, narrow)
    phi_imag = phi_imag.reshape(groups_z * planes, columns, narrow)
    phi_real, phi_imag = (
        lax.all_to_all(phi_real, "gz", split_axis=0, concat_axis=2, tiled=True),
        lax.all_to_all(phi_imag, "gz", split_axis=0, concat_axis=2, tiled=True),
    )
    zero_real = phi_real[:, 0]
    zero_imag = phi_imag[:, 0]
    joined_real = jnp.where(first, zero_real - phi_imag[:, -1], zero_real)
    joined_imag = jnp.where(first, zero_imag + phi_real[:, -1], zero_imag)
    phi_real = jnp.concatenate([joined_real[:, None], phi_real[:, 1:-1]], 1)
    phi_imag = jnp.concatenate([joined_imag[:, None], phi_imag[:, 1:-1]], 1)
    back_real = jnp.einsum("zxk,yk->zyx", phi_real, cos_y, precision=HIGHEST) - jnp.einsum(
        "zxk,yk->zyx", phi_imag, sin_y, precision=HIGHEST
    )
    back_imag = jnp.einsum("zxk,yk->zyx", phi_real, sin_y, precision=HIGHEST) + jnp.einsum(
        "zxk,yk->zyx", phi_imag, cos_y, precision=HIGHEST
    )
    back_real, back_imag = (
        lax.all_to_all(back_real, "gy", split_axis=1, concat_axis=2, tiled=True),
        lax.all_to_all(back_imag, "gy", split_axis=1, concat_axis=2, tiled=True),
    )
    potential = jnp.einsum(
        "kx,zyk->zyx", cos_x * weight_x, back_real, precision=HIGHEST
    ) - jnp.einsum("kx,zyk->zyx", sin_x * weight_x, back_imag, precision=HIGHEST)
    potential = potential * (1.0 / (width_x * width_y))
    return potential.reshape(planes, rows_y * width_x)


def solution(mesh):
    return jax.shard_map(
        on_device,
        mesh=mesh,
        in_specs=(P("gz", "gy"),),
        out_specs=P("gz", "gy"),
        check_vma=False,
    )
```

profile of v0, /device:TPU:0, one launch (start us, length us, event | category | flops | bytes accessed | tf_op | source)
XLA Modules:
  0.0 421.9 jit_solution(14964756322759798216)
XLA Ops:
  6.1 4.2 %all-to-all-start = ((f32[8,88,176]{1,0,2:T(8,128)}), f32[8,88,176]{1,0,2:T(8,128)S(1)}, u32[]{:S(2)}, u32[]{:S(2)}) async-start(f32[8,88,176]{1,0,2:T(8,128)} %copy.44), calls=%async_computation | async-start | bytes 1441792 | tf_op jit(solution)/shard_map/all_to_all | solution.py:109
  14.4 6.8 %all-to-all-done = f32[8,88,176]{1,0,2:T(8,128)S(1)} async-done(((f32[8,88,176]{1,0,2:T(8,128)}), f32[8,88,176]{1,0,2:T(8,128)S(1)}, u32[]{:S(2)}, u32[]{:S(2)}) %all-to-all-start) | async-done | bytes 495648 | tf_op jit(solution)/shard_map/all_to_all | solution.py:109
  21.2 4.0 all-to-all-start.1
  26.0 4.1 fusion.38
  30.1 5.5 %all-to-all-done.1 = f32[8,88,176]{1,0,2:T(8,128)S(1)} async-done(((f32[8,88,176]{1,0,2:T(8,128)}), f32[8,88,176]{1,0,2:T(8,128)S(1)}, u32[]{:S(2)}, u32[]{:S(2)}) %all-to-all-start.1) | async-done | bytes 495648 | tf_op jit(solution)/shard_map/all_to_all | solution.py:110
  36.5 4.4 %convolution_add_fusion.1 = f32[8,44,352]{2,1,0:T(8,128)S(1)} fusion(f32[8,44,352]{2,1,0:T(8,128)} %fusion.38, f32[8,352,44]{1,2,0:T(8,128)S(1)} %reshape.235), kind=kOutput, calls=%fused_computation.43 | convolution fusion | flops 524609536 | bytes 1486848 | tf_op jit(solution)/shard_map/zyx,yk->zxk/dot_general | solution.py:112
  40.9 3.4 fusion.36
  51.8 6.5 %all-to-all-start.2 = ((f32[8,1,15840]{2,1,0:T(1,128)}), f32[8,1,15840]{2,1,0:T(1,128)S(1)}, u32[]{:S(2)}, u32[]{:S(2)}) async-start(f32[8,1,15840]{2,1,0:T(1,128)} %reshape.238), calls=%async_computation.2 | async-start | bytes 1015808 | tf_op jit(solution)/shard_map/all_to_all | solution.py:138
  62.5 9.7 %all-to-all-done.2 = f32[8,1,15840]{2,1,0:T(1,128)S(1)} async-done(((f32[8,1,15840]{2,1,0:T(1,128)}), f32[8,1,15840]{2,1,0:T(1,128)S(1)}, u32[]{:S(2)}, u32[]{:S(2)}) %all-to-all-start.2) | async-done | bytes 506912 | tf_op jit(solution)/shard_map/all_to_all | solution.py:138
  72.2 3.9 all-to-all-start.3
  84.2 5.2 %copy.58 = f32[45,8,8,44]{2,1,3,0:T(8,128)} copy(f32[45,8,8,44]{0,2,3,1:T(8,128)S(1)} %bitcast.174) | data formatting | bytes 1013760
  93.7 5.2 %copy.59 = f32[45,8,8,44]{2,1,3,0:T(8,128)} copy(f32[45,8,8,44]{0,2,3,1:T(8,128)S(1)} %bitcast.176) | data formatting | bytes 1013760
  98.9 188.8 %while.15 = (s32[]{:T(128)}, f32[45,8,8,44]{2,1,3,0:T(8,128)}, f32[45,8,8,44]{2,1,3,0:T(8,128)}, f32[45,8,8,44]{2,1,3,0:T(8,128)}, f32[45,44]{1,0:T(8,128)S(1)}, /*index=5*/f32[45,8,8,44]{2,1,3,0:T(8,128)}, s32[]{:T(128)}) while((s32[]{:T(128)}, f32[45,8,8,44]{2,1,3,0:T(8,128)}, f32[45,8,8,44]{2,1,3,0:T(8,128)}, ...), condition=%wide.region_1.2_spmd.clone, body=%wide.region_0.1_spmd.clone.sunk | while | flops 546562 | bytes 724505 | solution.py:57
  303.9 18.4 %fusion.16 = (f32[8,8,45,44]{1,0,3,2:T(8,128)}, f32[8,8,45,44]{1,0,3,2:T(8,128)}) fusion(f32[45,8,8,44]{2,1,3,0:T(8,128)} %get-tuple-element.90, f32[8,45,44]{0,2,1:T(8,128)S(1)} %bitcast.188, f32[8,45,44]{0,2,1:T(8,128)} %bitcast.189, f32[45,44]{1,0:T(8,128)S(1)} %copy-done.7, f32[8,45,44]{0,2,1:T(8,128)S(1)} %copy-done, f32[8,45,44]{0,2,1:T(8,128)S(1)} %copy-done.1, ...), kind=kLoop, calls=%fused_computation.21 | loop fusion | flops 1267200 | bytes 2415600 | tf_op jit(solution)/shard_map/mul | solution.py:92
  322.3 7.6 %copy.120 = f32[8,8,45,44]{2,3,1,0:T(8,128)S(1)} copy(f32[8,8,45,44]{1,0,3,2:T(8,128)} %get-tuple-element.142) | data formatting | bytes 1013760 | tf_op jit(solution)/shard_map/reshape | solution.py:162
  332.3 5.3 %all-to-all-start.4 = ((f32[8,1,15840]{2,1,0:T(1,128)}), f32[8,1,15840]{2,1,0:T(1,128)S(1)}, u32[]{:S(2)}, u32[]{:S(2)}) async-start(f32[8,1,15840]{2,1,0:T(1,128)} %reshape.242), calls=%async_computation.4 | async-start | bytes 1015808 | tf_op jit(solution)/shard_map/all_to_all | solution.py:165
  337.7 7.6 %copy.122 = f32[8,8,45,44]{2,3,1,0:T(8,128)S(1)} copy(f32[8,8,45,44]{1,0,3,2:T(8,128)} %get-tuple-element.141) | data formatting | bytes 1013760 | tf_op jit(solution)/shard_map/reshape | solution.py:163
  347.7 3.5 all-to-all-done.4
  351.2 3.8 all-to-all-start.5
  360.2 8.4 %all-to-all-done.5 = f32[8,1,15840]{2,1,0:T(1,128)S(1)} async-done(((f32[8,1,15840]{2,1,0:T(1,128)}), f32[8,1,15840]{2,1,0:T(1,128)S(1)}, u32[]{:S(2)}, u32[]{:S(2)}) %all-to-all-start.5) | async-done | bytes 506912 | tf_op jit(solution)/shard_map/all_to_all | solution.py:166
  377.3 3.8 fusion.21
  384.4 3.5 all-to-all-start.6
  387.9 3.4 fusion.28
  397.9 3.6 all-to-all-start.7
  (304 shorter events, 289.2 us)
Async XLA Ops:
  6.1 15.2 %all-to-all-start = ((f32[8,88,176]{1,0,2:T(8,128)}), f32[8,88,176]{1,0,2:T(8,128)S(1)}, u32[]{:S(2)}, u32[]{:S(2)}) async-start(f32[8,88,176]{1,0,2:T(8,128)} %copy.44), calls=%async_computation | async-start | bytes 1441792 | tf_op jit(solution)/shard_map/all_to_all | solution.py:109
  10.3 3.0 copy-start.8
  10.3 3.0 copy-start.10
  21.2 14.4 %all-to-all-start.1 = ((f32[8,88,176]{1,0,2:T(8,128)}), f32[8,88,176]{1,0,2:T(8,128)S(1)}, u32[]{:S(2)}, u32[]{:S(2)}) async-start(f32[8,88,176]{1,0,2:T(8,128)} %copy.47), calls=%async_computation.1 | async-start | bytes 1441792 | tf_op jit(solution)/shard_map/all_to_all | solution.py:110
  51.8 20.4 %all-to-all-start.2 = ((f32[8,1,15840]{2,1,0:T(1,128)}), f32[8,1,15840]{2,1,0:T(1,128)S(1)}, u32[]{:S(2)}, u32[]{:S(2)}) async-start(f32[8,1,15840]{2,1,0:T(1,128)} %reshape.238), calls=%async_computation.2 | async-start | bytes 1015808 | tf_op jit(solution)/shard_map/all_to_all | solution.py:138
  72.2 17.9 %all-to-all-start.3 = ((f32[8,1,15840]{2,1,0:T(1,128)}), f32[8,1,15840]{2,1,0:T(1,128)S(1)}, u32[]{:S(2)}, u32[]{:S(2)}) async-start(f32[8,1,15840]{2,1,0:T(1,128)} %reshape.240), calls=%async_computation.3 | async-start | bytes 1015808 | tf_op jit(solution)/shard_map/all_to_all | solution.py:139
  290.2 2.5 copy-start.3
  290.2 2.5 copy-start.4
  299.9 4.0 copy-start
  299.9 4.0 copy-start.1
  299.9 4.0 copy-start.7
  332.3 18.9 %all-to-all-start.4 = ((f32[8,1,15840]{2,1,0:T(1,128)}), f32[8,1,15840]{2,1,0:T(1,128)S(1)}, u32[]{:S(2)}, u32[]{:S(2)}) async-start(f32[8,1,15840]{2,1,0:T(1,128)} %reshape.242), calls=%async_computation.4 | async-start | bytes 1015808 | tf_op jit(solution)/shard_map/all_to_all | solution.py:165
  351.2 17.4 %all-to-all-start.5 = ((f32[8,1,15840]{2,1,0:T(1,128)}), f32[8,1,15840]{2,1,0:T(1,128)S(1)}, u32[]{:S(2)}, u32[]{:S(2)}) async-start(f32[8,1,15840]{2,1,0:T(1,128)} %reshape.244), calls=%async_computation.5 | async-start | bytes 1015808 | tf_op jit(solution)/shard_map/all_to_all | solution.py:166
  359.2 9.4 %copy-start.2 = (f32[8,45,352]{2,1,0:T(8,128)}, f32[8,45,352]{2,1,0:T(8,128)S(1)}, u32[]{:S(2)}) copy-start(f32[8,45,352]{2,1,0:T(8,128)S(1)} %reshape.236) | copy-start | bytes 1520644
  372.3 1.6 copy-start.5
  381.6 6.2 %copy-start.6 = (f32[8,43,352]{2,1,0:T(8,128)S(1)}, f32[8,43,352]{2,1,0:T(8,128)}, u32[]{:S(2)}) copy-start(f32[8,43,352]{2,1,0:T(8,128)} %slice.78) | copy-start | bytes 1453060
  384.4 13.5 %all-to-all-start.6 = ((f32[4,1,30976]{2,1,0:T(1,128)}), f32[4,1,30976]{2,1,0:T(1,128)S(1)}, u32[]{:S(2)}, u32[]{:S(2)}) async-start(f32[4,1,30976]{2,1,0:T(1,128)} %reshape.246), calls=%async_computation.6 | async-start | bytes 991232 | tf_op jit(solution)/shard_map/all_to_all | solution.py:181
  397.9 12.0 %all-to-all-start.7 = ((f32[4,1,30976]{2,1,0:T(1,128)}), f32[4,1,30976]{2,1,0:T(1,128)S(1)}, u32[]{:S(2)}, u32[]{:S(2)}) async-start(f32[4,1,30976]{2,1,0:T(1,128)} %reshape.248), calls=%async_computation.7 | async-start | bytes 991232 | tf_op jit(solution)/shard_map/all_to_all | solution.py:182
  415.0 2.7 copy-start.9
  415.0 2.7 copy-start.11
where the time goes:
time: 430 us; the launch traced here: 422 us
  matrix products  228 us (53%)
  local copies, waits for them, and re-layouts  81.6 us (19%)
  other arithmetic  38.6 us (9%)
  waiting for transfers between devices  37.7 us (9%)
  starting transfers between devices  34.8 us (8%)
    dot_general x45, matrix products, per_row(): jnp.einsum('ijn,jn->in', kernel, row_real, precision=HIGHEST)  94.1 us
    dot_general x45, matrix products, per_row(): jnp.einsum('ijn,jn->in', kernel, row_imag, precision=HIGHEST)  94 us
    unnamed x48, local copies, waits for them, and re-layouts  36.2 us
    mul x1, other arithmetic, assemble(): phi_imag = (local[1] + lower * carried[1] + upper * carried[3]) * scale  18.4 us
    all_to_all x1, waiting for transfers between devices, on_device(): lax.all_to_all(hat_real, 'gz', split_axis=2, concat_axis=0, tiled=True)  9.75 us
  transfers between devices with their start and end apart: 8, of which 7 were waited for; matrix products, arithmetic and copies ran while one was open for 13% of the time, Pallas kernels for 0%

commit v1 on v0

v1 whole, which is shorter than its diff:
```python
import functools
import math

import jax
import jax.numpy as jnp
import numpy as np
from jax import lax
from jax.experimental import pallas as pl
from jax.experimental.pallas import tpu as pltpu
from jax.sharding import PartitionSpec as P

NX = 352
NY = 352
SCREEN = 128
LANES = 128
MESH = pl.DeviceIdType.MESH


def basis(length):
    j = np.arange(length)
    half = length // 2
    m = np.where(j <= half, j, j - half)
    angle = (m[:, None] * j[None, :] % length) * (2.0 * math.pi / length)
    rows = np.where(j[:, None] <= half, np.cos(angle), np.sin(angle))
    amp = np.where((j == 0) | (j == half), math.sqrt(1.0 / length), math.sqrt(2.0 / length))
    return rows * amp[:, None]


def split(value):
    high = value.astype(jnp.bfloat16)
    low = (value - high.astype(jnp.float32)).astype(jnp.bfloat16)
    return high, low


def dot3(a, b):
    dot = functools.partial(jnp.dot, preferred_element_type=jnp.float32)
    return dot(a[0], b[0]) + (dot(a[0], b[1]) + dot(a[1], b[0]))


def kappa_of(rows, first_row, lanes, first_lane):
    def wave(shape, axis, first, length):
        index = lax.broadcasted_iota(jnp.int32, shape, axis) + first
        index = jnp.where(index <= length // 2, index, index - length // 2)
        return index.astype(jnp.float32) * (2.0 * math.pi / length)

    wave_y = wave((rows, lanes), 0, first_row, NY)
    wave_x = wave((rows, lanes), 1, first_lane, NX)
    return jnp.sqrt(1.0 / (SCREEN * SCREEN) + wave_x * wave_x + wave_y * wave_y)


def kernel(planes, rows_y, gz, gy, part, density, fx, fx_low, ix, ix_low, fy, fy_low, iy, iy_low,
           out, rows_ref, slab, send, recv, hat, seg, total, edge, edge_all, carry, carry_all,
           back, send_sem, recv_sem, own_sem, edge_send, edge_recv, carry_send, carry_recv,
           back_send, back_recv):
    width = NX // gy
    pad = LANES
    me_z = lax.axis_index("gz")
    me_y = lax.axis_index("gy")
    barrier = pltpu.get_barrier_semaphore()
    for i in range(1, gy):
        pl.semaphore_signal(barrier, inc=1, device_id=(me_z, lax.rem(me_y + i, gy)), device_id_type=MESH)
    for i in range(1, gz):
        pl.semaphore_signal(barrier, inc=1, device_id=(lax.rem(me_z + i, gz), me_y), device_id_type=MESH)

    period = LANES // math.gcd(NX, LANES)
    stretch = period * NX
    steps = rows_y // period
    tall = rows_y * planes
    chunks = [min(LANES, NX - c) for c in range(0, NX, LANES)]

    def unpack(t, _):
        base = pl.multiple_of(t * stretch, LANES)
        values = density[:, pl.ds(base, stretch)]
        for q in range(period):
            row = pl.multiple_of((t * period + q) * planes, planes)
            for c, size in enumerate(chunks):
                start = q * NX + c * LANES
                rows_ref[pl.ds(c * tall + row, planes), :size] = values[:, start:start + size]
        return 0

    lax.fori_loop(0, steps, unpack, 0)
    for z in range(planes):
        for c, size in enumerate(chunks):
            slab[z * rows_y:(z + 1) * rows_y, c * LANES:c * LANES + size] = rows_ref[
                pl.ds(c * tall + z, rows_y, stride=planes), :][:, :size]
    group = 2
    for z0 in range(0, planes, group):
        block = slab[z0 * rows_y:(z0 + group) * rows_y, :NX]
        result = dot3(split(block), (fx[...], fx_low[...]))
        for z in range(z0, z0 + group):
            for p in range(gy):
                send[p, :, z * width:(z + 1) * width] = result[
                    (z - z0) * rows_y:(z - z0 + 1) * rows_y, p * pad:p * pad + width]

    pl.semaphore_wait(barrier, gy - 1 + gz - 1)

    def exchange(source, target, sems, recvs):
        copies = []
        for i in list(range(2, gy)) + [1]:
            peer = lax.rem(me_y + i, gy)
            copy = pltpu.make_async_remote_copy(
                src_ref=source.at[peer], dst_ref=target.at[me_y],
                send_sem=sems.at[i], recv_sem=recvs.at[i],
                device_id=(me_z, peer), device_id_type=MESH)
            copy.start()
            copies.append(copy)
        own = pltpu.make_async_copy(source.at[me_y], target.at[me_y], own_sem)
        own.start()
        own.wait()
        for copy in copies:
            copy.wait()

    exchange(send, recv, send_sem, recv_sem)

    lanes = planes * width
    hat[...] = dot3((fy[...], fy_low[...]), split(recv[...].reshape(gy * rows_y, lanes)))
    rows = gz * part
    kappa = kappa_of(rows, 0, width, me_y * width)
    decay = jnp.exp(-kappa)
    value = None
    for z in range(planes):
        plane = hat[:, z * width:(z + 1) * width]
        seg[z] = plane
        value = plane if z == 0 else decay * value + plane
    edge[0] = value
    for z in range(planes - 1, -1, -1):
        value = seg[z] if z == planes - 1 else decay * value + seg[z]
    edge[1] = value

    copies = []
    mine = pl.ds(pl.multiple_of(me_z * part, part), part)
    for i in range(1, gz):
        peer = lax.rem(me_z + i, gz)
        copy = pltpu.make_async_remote_copy(
            src_ref=edge.at[:, pl.ds(pl.multiple_of(peer * part, part), part)],
            dst_ref=edge_all.at[me_z],
            send_sem=edge_send.at[i], recv_sem=edge_recv.at[i],
            device_id=(peer, me_y), device_id_type=MESH)
        copy.start()
        copies.append(copy)
    edge_all[me_z] = edge[:, mine]
    far = jnp.exp(-float(planes) * kappa_of(part, me_z * part, width, me_y * width))
    for copy in copies:
        copy.wait()
    value = jnp.zeros((part, width), jnp.float32)
    for s in range(gz):
        carry[s, 0] = value
        value = far * value + edge_all[s, 0]
    value = jnp.zeros((part, width), jnp.float32)
    for s in range(gz - 1, -1, -1):
        carry[s, 1] = value
        value = far * value + edge_all[s, 1]
    copies = []
    for i in range(1, gz):
        peer = lax.rem(me_z + i, gz)
        copy = pltpu.make_async_remote_copy(
            src_ref=carry.at[peer], dst_ref=carry_all.at[:, mine],
            send_sem=carry_send.at[i], recv_sem=carry_recv.at[i],
            device_id=(peer, me_y), device_id_type=MESH)
        copy.start()
        copies.append(copy)
    carry_all[:, mine] = carry[me_z]
    for copy in copies:
        copy.wait()

    scale = 0.5 / kappa
    value = carry_all[0]
    for z in range(planes):
        value = decay * value + seg[z]
        total[z] = value
    value = carry_all[1]
    for z in range(planes - 1, -1, -1):
        value = decay * value
        hat[:, z * width:(z + 1) * width] = (total[z] + value) * scale
        value = value + seg[z]

    result = dot3((iy[...], iy_low[...]), split(hat[...]))
    for p in range(gy):
        send[p] = result[p * rows_y:(p + 1) * rows_y]
    exchange(send, back, back_send, back_recv)

    slab[...] = jnp.zeros_like(slab)
    for z in range(planes):
        for p in range(gy):
            slab[z * rows_y:(z + 1) * rows_y, p * pad:p * pad + width] = back[
                p, :, z * width:(z + 1) * width]
    for z0 in range(0, planes, group):
        block = slab[z0 * rows_y:(z0 + group) * rows_y, :]
        result = dot3(split(block), (ix[...], ix_low[...]))
        for z in range(z0, z0 + group):
            for c in range(len(chunks)):
                rows_ref[pl.ds(c * tall + z, rows_y, stride=planes), :] = result[
                    (z - z0) * rows_y:(z - z0 + 1) * rows_y, c * LANES:(c + 1) * LANES]

    def pack(t, _):
        pieces = []
        for q in range(period):
            row = pl.multiple_of((t * period + q) * planes, planes)
            for c, size in enumerate(chunks):
                pieces.append(rows_ref[pl.ds(c * tall + row, planes), :][:, :size])
        base = pl.multiple_of(t * stretch, LANES)
        out[:, pl.ds(base, stretch)] = jnp.concatenate(pieces, axis=1)
        return 0

    lax.fori_loop(0, steps, pack, 0)


def on_device(density):
    planes = density.shape[0]
    gz = lax.axis_size("gz")
    gy = lax.axis_size("gy")
    rows_y = NY // gy
    width = NX // gy
    part = -(-NY // (8 * gz)) * 8
    rows = part * gz
    forward_x = np.zeros((NX, gy, LANES))
    forward_x[:, :, :width] = basis(NX).T.reshape(NX, gy, width)
    forward_x = forward_x.reshape(NX, gy * LANES)
    forward_y = np.zeros((rows, NY))
    forward_y[:NY] = basis(NY)
    tables = []
    inverse_x = np.zeros((gy * LANES, -(-NX // LANES) * LANES))
    inverse_x[:, :NX] = forward_x.T
    for table in (forward_x, inverse_x, forward_y, forward_y.T):
        table = table.astype(np.float32)
        high = table.astype(jnp.bfloat16)
        low = (table - high.astype(np.float32)).astype(jnp.bfloat16)
        tables += [high, low]
    f32 = jnp.float32
    vmem = pltpu.VMEM
    dma = pltpu.SemaphoreType.DMA
    lanes = planes * width
    spec = pl.BlockSpec(memory_space=pltpu.VMEM)
    return pl.pallas_call(
        functools.partial(kernel, planes, rows_y, gz, gy, part),
        out_shape=jax.ShapeDtypeStruct(density.shape, f32),
        in_specs=[spec] * (1 + len(tables)),
        out_specs=spec,
        scratch_shapes=[
            vmem((-(-NX // LANES) * rows_y * planes, LANES), f32),
            vmem((rows_y * planes, gy * LANES), f32),
            vmem((gy, rows_y, lanes), f32),
            vmem((gy, rows_y, lanes), f32),
            vmem((rows, lanes), f32),
            vmem((planes, rows, width), f32),
            vmem((planes, rows, width), f32),
            vmem((2, rows, width), f32),
            vmem((gz, 2, part, width), f32),
            vmem((gz, 2, part, width), f32),
            vmem((2, rows, width), f32),
            vmem((gy, rows_y, lanes), f32),
            dma((gy,)), dma((gy,)), dma(()),
            dma((gz,)), dma((gz,)), dma((gz,)), dma((gz,)),
            dma((gy,)), dma((gy,)),
        ],
        compiler_params=pltpu.CompilerParams(
            collective_id=0, has_side_effects=True, vmem_limit_bytes=60 * 1024 * 1024),
    )(density, *tables)


def solution(mesh):
    return jax.shard_map(
        on_device,
        mesh=mesh,
        in_specs=(P("gz", "gy"),),
        out_specs=P("gz", "gy"),
        check_vma=False,
    )
```

time: 430 us -> 63.9 us (0.15)
  the two profiles are of different devices: /device:TPU:0 before, /device:TPU:31 now
where the time goes in v1:
time: 63.9 us; the launch traced here: 63.7 us
  Pallas kernels  61.5 us (96%)
  local copies, waits for them, and re-layouts  2.22 us (3%)
    pallas_call x1, Pallas kernels, on_device(): pl.pallas_call(functools.partial(kernel, planes, rows_y, gz, gy, part), o...  61.5 us
    unnamed x1, local copies, waits for them, and re-layouts  2.22 us

profile of v1, /device:TPU:31, one launch (start us, length us, event | category | flops | bytes accessed | tf_op | source)
XLA Modules:
  0.0 63.7 jit_solution(4999283659411093551)
XLA Ops:
  0.0 61.5 %shard_map.91 = f32[8,30976]{1,0:T(8,128)} custom-call(f32[8,30976]{1,0:T(8,128)} %density.1, bf16[352,512]{1,0:T(8,128)(2,1)} %constant.16.clone.fx, bf16[352,512]{1,0:T(8,128)(2,1)} %constant.17.clone.fx_low, bf16[512,384]{1,0:T(8,128)(2,1)} %constant.18.clone.ix, bf16[512,384]{1,0:T(8,128)(2,1)} %constant.19.clone.ix_low, ...), custom_call_target="tpu_custom_call" | custom-call | tf_op jit(solution)/shard_map/pallas_call | solution.py:234
  61.5 2.2 %copy.11 = f32[8,30976]{1,0:T(8,128)} copy(f32[8,30976]{1,0:T(8,128)} %shard_map.91) | data formatting | bytes 1982464

commit v2 on v1

v2 whole, which is shorter than its diff:
```python
import functools
import math

import jax
import jax.numpy as jnp
import numpy as np
from jax import lax
from jax.experimental import pallas as pl
from jax.experimental.pallas import tpu as pltpu
from jax.sharding import PartitionSpec as P

NX = 352
NY = 352
SCREEN = 128
LANES = 128
MESH = pl.DeviceIdType.MESH


def basis(length):
    j = np.arange(length)
    half = length // 2
    m = np.where(j <= half, j, j - half)
    angle = (m[:, None] * j[None, :] % length) * (2.0 * math.pi / length)
    rows = np.where(j[:, None] <= half, np.cos(angle), np.sin(angle))
    amp = np.where((j == 0) | (j == half), math.sqrt(1.0 / length), math.sqrt(2.0 / length))
    return rows * amp[:, None]


def split(value):
    high = value.astype(jnp.bfloat16)
    low = (value - high.astype(jnp.float32)).astype(jnp.bfloat16)
    return high, low


def dot3(a, b):
    dot = functools.partial(jnp.dot, preferred_element_type=jnp.float32)
    return dot(a[0], b[0]) + (dot(a[0], b[1]) + dot(a[1], b[0]))


def kappa_of(rows, first_row, lanes, first_lane):
    def wave(shape, axis, first, length):
        index = lax.broadcasted_iota(jnp.int32, shape, axis) + first
        index = jnp.where(index <= length // 2, index, index - length // 2)
        return index.astype(jnp.float32) * (2.0 * math.pi / length)

    wave_y = wave((rows, lanes), 0, first_row, NY)
    wave_x = wave((rows, lanes), 1, first_lane, NX)
    return jnp.sqrt(1.0 / (SCREEN * SCREEN) + wave_x * wave_x + wave_y * wave_y)


def kernel(planes, rows_y, gz, gy, part, parts, density, *refs):
    tables_hbm, refs = refs[:8], refs[8:]
    (out, rows_ref, slab, cols, acc, out_buf, send, recv, hat, seg, total, edge, edge_all, carry,
     carry_all, send_back, back, decay_ref, scale_ref, *refs) = refs
    tables, refs = refs[:8], refs[8:]
    (table_sem, own_sem, out_sem, send_sem, recv_sem, edge_send, edge_recv, carry_send, carry_recv,
     back_send, back_recv) = refs
    fx, fx_low, ix, ix_low, fy, fy_low, iy, iy_low = tables
    half = NX // gy // parts
    slot = LANES // parts
    me_z = lax.axis_index("gz")
    me_y = lax.axis_index("gy")
    loads = []
    for i in range(8):
        load = pltpu.make_async_copy(tables_hbm[i], tables[i], table_sem.at[i])
        load.start()
        loads.append(load)
    barrier = pltpu.get_barrier_semaphore()
    for i in range(1, gy):
        pl.semaphore_signal(barrier, inc=1, device_id=(me_z, lax.rem(me_y + i, gy)), device_id_type=MESH)
    for i in range(1, gz):
        pl.semaphore_signal(barrier, inc=1, device_id=(lax.rem(me_z + i, gz), me_y), device_id_type=MESH)

    period = LANES // math.gcd(NX, LANES)
    stretch = period * NX
    steps = rows_y // period
    tall = rows_y * planes
    chunks = [min(LANES, NX - c) for c in range(0, NX, LANES)]

    def unpack(t, _):
        base = pl.multiple_of(t * stretch, LANES)
        values = density[:, pl.ds(base, stretch)]
        for q in range(period):
            row = pl.multiple_of((t * period + q) * planes, planes)
            for c, size in enumerate(chunks):
                start = q * NX + c * LANES
                rows_ref[pl.ds(c * tall + row, planes), :size] = values[:, start:start + size]
        return 0

    lax.fori_loop(0, steps, unpack, 0)
    for z in range(planes):
        for c, size in enumerate(chunks):
            slab[z * rows_y:(z + 1) * rows_y, c * LANES:c * LANES + size] = rows_ref[
                pl.ds(c * tall + z, rows_y, stride=planes), :][:, :size]
    group = 2
    mine = pl.ds(pl.multiple_of(me_z * part, part), part)

    def forward_x(h):
        for z0 in range(0, planes, group):
            block = slab[z0 * rows_y:(z0 + group) * rows_y, :NX]
            result = dot3(split(block), (fx[h], fx_low[h]))
            for z in range(z0, z0 + group):
                for p in range(gy):
                    send[h, p, :, z * half:(z + 1) * half] = result[
                        (z - z0) * rows_y:(z - z0 + 1) * rows_y, p * slot:p * slot + half]

    def exchange(source, target, h, sems, recvs):
        copies = []
        for i in list(range(2, gy)) + [1]:
            peer = lax.rem(me_y + i, gy)
            copy = pltpu.make_async_remote_copy(
                src_ref=source.at[h, peer], dst_ref=target.at[h, me_y],
                send_sem=sems.at[h, i], recv_sem=recvs.at[h, i],
                device_id=(me_z, peer), device_id_type=MESH)
            copy.start()
            copies.append(copy)
        own = pltpu.make_async_copy(source.at[h, me_y], target.at[h, me_y], own_sem)
        own.start()
        own.wait()
        return copies

    def arrive(copies):
        for copy in copies:
            copy.wait()

    def edges(h):
        lanes = planes * half
        hat[...] = dot3((fy[...], fy_low[...]), split(recv[h].reshape(gy * rows_y, lanes)))
        decay = decay_ref[h]
        value = None
        for z in range(planes):
            plane = hat[:, z * half:(z + 1) * half]
            seg[h, z] = plane
            value = plane if z == 0 else decay * value + plane
        edge[h, :, :half] = value
        for z in range(planes - 1, -1, -1):
            value = seg[h, z] if z == planes - 1 else decay * value + seg[h, z]
        edge[h, :, half:2 * half] = value
        copies = []
        for i in range(1, gz):
            peer = lax.rem(me_z + i, gz)
            copy = pltpu.make_async_remote_copy(
                src_ref=edge.at[h, pl.ds(pl.multiple_of(peer * part, part), part)],
                dst_ref=edge_all.at[h, me_z],
                send_sem=edge_send.at[h, i], recv_sem=edge_recv.at[h, i],
                device_id=(peer, me_y), device_id_type=MESH)
            copy.start()
            copies.append(copy)
        edge_all[h, me_z] = edge[h, mine]
        return copies

    def carries(h):
        far = kappa_of(part, me_z * part, half, (me_y * parts + h) * half)
        far = jnp.exp(-float(planes) * far)
        value = jnp.zeros((part, half), jnp.float32)
        for s in range(gz):
            carry[h, s, :, :half] = value
            value = far * value + edge_all[h, s, :, :half]
        value = jnp.zeros((part, half), jnp.float32)
        for s in range(gz - 1, -1, -1):
            carry[h, s, :, half:2 * half] = value
            value = far * value + edge_all[h, s, :, half:2 * half]
        copies = []
        for i in range(1, gz):
            peer = lax.rem(me_z + i, gz)
            copy = pltpu.make_async_remote_copy(
                src_ref=carry.at[h, peer], dst_ref=carry_all.at[h, mine],
                send_sem=carry_send.at[h, i], recv_sem=carry_recv.at[h, i],
                device_id=(peer, me_y), device_id_type=MESH)
            copy.start()
            copies.append(copy)
        carry_all[h, mine] = carry[h, me_z]
        return copies

    def inverse_y(h):
        decay = decay_ref[h]
        scale = scale_ref[h]
        value = carry_all[h, :, :half]
        for z in range(planes):
            value = decay * value + seg[h, z]
            total[z] = value
        value = carry_all[h, :, half:2 * half]
        for z in range(planes - 1, -1, -1):
            value = decay * value
            hat[:, z * half:(z + 1) * half] = (total[z] + value) * scale
            value = value + seg[h, z]
        result = dot3((iy[...], iy_low[...]), split(hat[...]))
        for p in range(gy):
            send_back[h, p] = result[p * rows_y:(p + 1) * rows_y]

    def inverse_x(h):
        for z0 in range(0, planes, group):
            for z in range(z0, z0 + group):
                for p in range(gy):
                    cols[z * rows_y:(z + 1) * rows_y, p * slot:p * slot + half] = back[
                        h, p, :, z * half:(z + 1) * half]
            block = pl.ds(z0 * rows_y, group * rows_y)
            result = dot3(split(cols[block, :]), (ix[h], ix_low[h]))
            if h > 0:
                result = result + acc[block, :]
            if h < parts - 1:
                acc[block, :] = result
                continue
            for z in range(z0, z0 + group):
                for c in range(len(chunks)):
                    rows_ref[pl.ds(c * tall + z, rows_y, stride=planes), :] = result[
                        (z - z0) * rows_y:(z - z0 + 1) * rows_y, c * LANES:(c + 1) * LANES]

    loads[0].wait()
    loads[1].wait()
    moving = []
    for h in range(parts):
        forward_x(h)
        if h == 0:
            pl.semaphore_wait(barrier, gy - 1 + gz - 1)
        moving.append(exchange(send, recv, h, send_sem, recv_sem))
    for h in range(parts):
        kappa = kappa_of(gz * part, 0, half, (me_y * parts + h) * half)
        decay_ref[h] = jnp.exp(-kappa)
        scale_ref[h] = 0.5 / kappa
    edge[...] = jnp.zeros_like(edge)
    carry[...] = jnp.zeros_like(carry)
    cols[...] = jnp.zeros_like(cols)
    for i in range(2, 8):
        loads[i].wait()
    sent = []
    for h in range(parts):
        arrive(moving[h])
        sent.append(edges(h))
    returned = []
    for h in range(parts):
        arrive(sent[h])
        returned.append(carries(h))
    moving = []
    for h in range(parts):
        arrive(returned[h])
        inverse_y(h)
        moving.append(exchange(send_back, back, h, back_send, back_recv))
    for h in range(parts):
        arrive(moving[h])
        inverse_x(h)

    def pack(t, _):
        pieces = []
        for q in range(period):
            row = pl.multiple_of((t * period + q) * planes, planes)
            for c, size in enumerate(chunks):
                pieces.append(rows_ref[pl.ds(c * tall + row, planes), :][:, :size])
        base = pl.multiple_of(t * stretch, LANES)
        out_buf[:, pl.ds(base, stretch)] = jnp.concatenate(pieces, axis=1)
        return 0

    stores = []
    cuts = [0, steps // 2, steps]
    for i in range(2):
        lax.fori_loop(cuts[i], cuts[i + 1], pack, 0)
        span = pl.ds(cuts[i] * stretch, (cuts[i + 1] - cuts[i]) * stretch)
        store = pltpu.make_async_copy(out_buf.at[:, span], out.at[:, span], out_sem.at[i])
        store.start()
        stores.append(store)
    for store in stores:
        store.wait()


def on_device(density):
    planes = density.shape[0]
    gz = lax.axis_size("gz")
    gy = lax.axis_size("gy")
    parts = 2
    rows_y = NY // gy
    half = NX // gy // parts
    slot = LANES // parts
    part = -(-NY // (8 * gz)) * 8
    rows = part * gz
    wide = -(-NX // LANES) * LANES
    forward_x = np.zeros((parts, NX, gy, slot))
    forward_x[..., :half] = basis(NX).T.reshape(NX, gy, parts, half).transpose(2, 0, 1, 3)
    forward_x = forward_x.reshape(parts, NX, gy * slot)
    inverse_x = np.zeros((parts, gy * slot, wide))
    inverse_x[..., :NX] = forward_x.transpose(0, 2, 1)
    forward_y = np.zeros((rows, NY))
    forward_y[:NY] = basis(NY)
    tables = []
    for table in (forward_x, inverse_x, forward_y, forward_y.T):
        table = table.astype(np.float32)
        high = table.astype(jnp.bfloat16)
        low = (table - high.astype(np.float32)).astype(jnp.bfloat16)
        tables += [high, low]
    f32 = jnp.float32
    vmem = pltpu.VMEM
    dma = pltpu.SemaphoreType.DMA
    lanes = planes * half
    spec = pl.BlockSpec(memory_space=pltpu.VMEM)
    free = pl.BlockSpec(memory_space=pl.ANY)
    return pl.pallas_call(
        functools.partial(kernel, planes, rows_y, gz, gy, part, parts),
        out_shape=jax.ShapeDtypeStruct(density.shape, f32),
        in_specs=[spec] + [free] * len(tables),
        out_specs=free,
        scratch_shapes=[
            vmem((wide // LANES * rows_y * planes, LANES), f32),
            vmem((rows_y * planes, wide), f32),
            vmem((rows_y * planes, gy * slot), f32),
            vmem((rows_y * planes, wide), f32),
            vmem(density.shape, f32),
            vmem((parts, gy, rows_y, lanes), f32),
            vmem((parts, gy, rows_y, lanes), f32),
            vmem((rows, lanes), f32),
            vmem((parts, planes, rows, half), f32),
            vmem((planes, rows, half), f32),
            vmem((parts, rows, LANES), f32),
            vmem((parts, gz, part, LANES), f32),
            vmem((parts, gz, part, LANES), f32),
            vmem((parts, rows, LANES), f32),
            vmem((parts, gy, rows_y, lanes), f32),
            vmem((parts, gy, rows_y, lanes), f32),
            vmem((parts, rows, half), f32),
            vmem((parts, rows, half), f32),
            *[vmem(table.shape, jnp.bfloat16) for table in tables],
            dma((8,)), dma(()), dma((2,)),
            *[dma((parts, gy))] * 2,
            *[dma((parts, gz))] * 4,
            *[dma((parts, gy))] * 2,
        ],
        compiler_params=pltpu.CompilerParams(
            collective_id=0, has_side_effects=True, vmem_limit_bytes=60 * 1024 * 1024),
    )(density, *tables)


def solution(mesh):
    return jax.shard_map(
        on_device,
        mesh=mesh,
        in_specs=(P("gz", "gy"),),
        out_specs=P("gz", "gy"),
        check_vma=False,
    )
```

time: 63.9 us -> 53.8 us (0.84)
  the two profiles are of different devices: /device:TPU:31 before, /device:TPU:0 now
where the time goes in v2:
time: 53.8 us; the launch traced here: 52.8 us
  Pallas kernels  50.6 us (94%)
  local copies, waits for them, and re-layouts  2.22 us (4%)
    pallas_call x1, Pallas kernels, on_device(): pl.pallas_call(functools.partial(kernel, planes, rows_y, gz, gy, part, pa...  50.6 us
    unnamed x1, local copies, waits for them, and re-layouts  2.22 us

profile of v2, /device:TPU:0, one launch (start us, length us, event | category | flops | bytes accessed | tf_op | source)
XLA Modules:
  0.0 52.8 jit_solution(16887854380939472299)
XLA Ops:
  0.0 50.6 %shard_map.91 = f32[8,30976]{1,0:T(8,128)} custom-call(f32[8,30976]{1,0:T(8,128)} %density.1, bf16[2,352,256]{2,1,0:T(8,128)(2,1)} %constant.16.clone.refs_0_, bf16[2,352,256]{2,1,0:T(8,128)(2,1)} %constant.17.clone.refs_1_, bf16[2,256,384]{2,1,0:T(8,128)(2,1)} %constant.18.clone.refs_2_, bf16[2,256,384]{2,1,0:T(8,128)(2,1)} %constant.19.clone.refs_3_, ...), custom_call_target="tpu_custom_call" | custom-call | tf_op jit(solution)/shard_map/pallas_call | solution.py:295
  50.6 2.2 %copy.11 = f32[8,30976]{1,0:T(8,128)} copy(f32[8,30976]{1,0:T(8,128)} %shard_map.91) | data formatting | bytes 1982464

commit v3 on v2

--- a/solution.py
+++ b/solution.py
@@ -37,27 +37,33 @@
     return dot(a[0], b[0]) + (dot(a[0], b[1]) + dot(a[1], b[0]))
 
 
-def kappa_of(rows, first_row, lanes, first_lane):
-    def wave(shape, axis, first, length):
-        index = lax.broadcasted_iota(jnp.int32, shape, axis) + first
+def kappa_at(row, column):
+    def wave(index, length):
         index = jnp.where(index <= length // 2, index, index - length // 2)
         return index.astype(jnp.float32) * (2.0 * math.pi / length)
 
-    wave_y = wave((rows, lanes), 0, first_row, NY)
-    wave_x = wave((rows, lanes), 1, first_lane, NX)
+    wave_y = wave(row, NY)
+    wave_x = wave(column, NX)
     return jnp.sqrt(1.0 / (SCREEN * SCREEN) + wave_x * wave_x + wave_y * wave_y)
+
+
+def kappa_of(rows, first_row, lanes, first_lane):
+    row = lax.broadcasted_iota(jnp.int32, (rows, lanes), 0) + first_row
+    column = lax.broadcasted_iota(jnp.int32, (rows, lanes), 1) + first_lane
+    return kappa_at(row, column)
 
 
 def kernel(planes, rows_y, gz, gy, part, parts, density, *refs):
     tables_hbm, refs = refs[:8], refs[8:]
     (out, rows_ref, slab, cols, acc, out_buf, send, recv, hat, seg, total, edge, edge_all, carry,
-     carry_all, send_back, back, decay_ref, scale_ref, *refs) = refs
+     carry_all, ends, send_back, back, decay_ref, scale_ref, *refs) = refs
     tables, refs = refs[:8], refs[8:]
     (table_sem, own_sem, out_sem, send_sem, recv_sem, edge_send, edge_recv, carry_send, carry_recv,
      back_send, back_recv) = refs
     fx, fx_low, ix, ix_low, fy, fy_low, iy, iy_low = tables
-    half = NX // gy // parts
-    slot = LANES // parts
+    width = NX // gy
+    half = slot = LANES // 4
+    fold = part // 2
     me_z = lax.axis_index("gz")
     me_y = lax.axis_index("gy")
     loads = []
@@ -93,7 +99,21 @@
             slab[z * rows_y:(z + 1) * rows_y, c * LANES:c * LANES + size] = rows_ref[
                 pl.ds(c * tall + z, rows_y, stride=planes), :][:, :size]
     group = 2
-    mine = pl.ds(pl.multiple_of(me_z * part, part), part)
+
+    def fill(h, which, value):
+        for o in range(gz):
+            for k in range(2):
+                lane = (2 * k + which) * half
+                row = o * part + k * fold
+                edge[h, o, :, lane:lane + half] = value[row:row + fold]
+
+    def take(h, which):
+        for o in range(gz):
+            for k in range(2):
+                lane = (2 * k + which) * half
+                row = o * part + k * fold
+                ends[which, row:row + fold] = carry_all[h, o, :, lane:lane + half]
+        return ends[which]
 
     def forward_x(h):
         for z0 in range(0, planes, group):
@@ -132,54 +152,57 @@
             plane = hat[:, z * half:(z + 1) * half]
             seg[h, z] = plane
             value = plane if z == 0 else decay * value + plane
-        edge[h, :, :half] = value
+        fill(h, 0, value)
         for z in range(planes - 1, -1, -1):
             value = seg[h, z] if z == planes - 1 else decay * value + seg[h, z]
-        edge[h, :, half:2 * half] = value
+        fill(h, 1, value)
         copies = []
         for i in range(1, gz):
             peer = lax.rem(me_z + i, gz)
             copy = pltpu.make_async_remote_copy(
-                src_ref=edge.at[h, pl.ds(pl.multiple_of(peer * part, part), part)],
+                src_ref=edge.at[h, peer],
                 dst_ref=edge_all.at[h, me_z],
                 send_sem=edge_send.at[h, i], recv_sem=edge_recv.at[h, i],
                 device_id=(peer, me_y), device_id_type=MESH)
             copy.start()
             copies.append(copy)
-        edge_all[h, me_z] = edge[h, mine]
+        edge_all[h, me_z] = edge[h, me_z]
         return copies
 
     def carries(h):
-        far = kappa_of(part, me_z * part, half, (me_y * parts + h) * half)
-        far = jnp.exp(-float(planes) * far)
-        value = jnp.zeros((part, half), jnp.float32)
+        lane = lax.broadcasted_iota(jnp.int32, (fold, LANES), 1)
+        row = lax.broadcasted_iota(jnp.int32, (fold, LANES), 0) + me_z * part
+        row = jnp.where(lane >= 2 * half, row + fold, row)
+        upward = (lane % (2 * half)) < half
+        far = jnp.exp(-float(planes) * kappa_at(row, me_y * width + h * half + lane % half))
+        value = jnp.zeros((fold, LANES), jnp.float32)
         for s in range(gz):
-            carry[h, s, :, :half] = value
-            value = far * value + edge_all[h, s, :, :half]
-        value = jnp.zeros((part, half), jnp.float32)
+            carry[h, s] = value
+            value = far * value + edge_all[h, s]
+        value = jnp.zeros((fold, LANES), jnp.float32)
         for s in range(gz - 1, -1, -1):
-            carry[h, s, :, half:2 * half] = value
-            value = far * value + edge_all[h, s, :, half:2 * half]
+            carry[h, s] = jnp.where(upward, carry[h, s], value)
+            value = far * value + edge_all[h, s]
         copies = []
         for i in range(1, gz):
             peer = lax.rem(me_z + i, gz)
             copy = pltpu.make_async_remote_copy(
-                src_ref=carry.at[h, peer], dst_ref=carry_all.at[h, mine],
+                src_ref=carry.at[h, peer], dst_ref=carry_all.at[h, me_z],
                 send_sem=carry_send.at[h, i], recv_sem=carry_recv.at[h, i],
                 device_id=(peer, me_y), device_id_type=MESH)
             copy.start()
             copies.append(copy)
-        carry_all[h, mine] = carry[h, me_z]
+        carry_all[h, me_z] = carry[h, me_z]
         return copies
 
     def inverse_y(h):
         decay = decay_ref[h]
         scale = scale_ref[h]
-        value = carry_all[h, :, :half]
+        value = take(h, 0)
         for z in range(planes):
             value = decay * value + seg[h, z]
             total[z] = value
-        value = carry_all[h, :, half:2 * half]
+        value = take(h, 1)
         for z in range(planes - 1, -1, -1):
             value = decay * value
             hat[:, z * half:(z + 1) * half] = (total[z] + value) * scale
@@ -215,12 +238,9 @@
             pl.semaphore_wait(barrier, gy - 1 + gz - 1)
         moving.append(exchange(send, recv, h, send_sem, recv_sem))
     for h in range(parts):
-        kappa = kappa_of(gz * part, 0, half, (me_y * parts + h) * half)
+        kappa = kappa_of(gz * part, 0, half, me_y * width + h * half)
         decay_ref[h] = jnp.exp(-kappa)
         scale_ref[h] = 0.5 / kappa
-    edge[...] = jnp.zeros_like(edge)
-    carry[...] = jnp.zeros_like(carry)
-    cols[...] = jnp.zeros_like(cols)
     for i in range(2, 8):
         loads[i].wait()
     sent = []
@@ -266,15 +286,16 @@
     planes = density.shape[0]
     gz = lax.axis_size("gz")
     gy = lax.axis_size("gy")
-    parts = 2
     rows_y = NY // gy
-    half = NX // gy // parts
-    slot = LANES // parts
-    part = -(-NY // (8 * gz)) * 8
+    width = NX // gy
+    half = slot = LANES // 4
+    parts = -(-width // half)
+    part = -(-NY // (16 * gz)) * 16
     rows = part * gz
     wide = -(-NX // LANES) * LANES
-    forward_x = np.zeros((parts, NX, gy, slot))
-    forward_x[..., :half] = basis(NX).T.reshape(NX, gy, parts, half).transpose(2, 0, 1, 3)
+    forward_x = np.zeros((NX, gy, parts * half))
+    forward_x[:, :, :width] = basis(NX).T.reshape(NX, gy, width)
+    forward_x = forward_x.reshape(NX, gy, parts, half).transpose(2, 0, 1, 3)
     forward_x = forward_x.reshape(parts, NX, gy * slot)
     inverse_x = np.zeros((parts, gy * slot, wide))
     inverse_x[..., :NX] = forward_x.transpose(0, 2, 1)
@@ -308,10 +329,8 @@
             vmem((rows, lanes), f32),
             vmem((parts, planes, rows, half), f32),
             vmem((planes, rows, half), f32),
-            vmem((parts, rows, LANES), f32),
-            vmem((parts, gz, part, LANES), f32),
-            vmem((parts, gz, part, LANES), f32),
-            vmem((parts, rows, LANES), f32),
+            *[vmem((parts, gz, part // 2, LANES), f32)] * 4,
+            vmem((2, rows, half), f32),
             vmem((parts, gy, rows_y, lanes), f32),
             vmem((parts, gy, rows_y, lanes), f32),
             vmem((parts, rows, half), f32),

time: 53.8 us -> 49.5 us (0.920); the launches traced: 52.8 us -> 49.3 us
  Pallas kernels: 50.6 us -> 47.1 us
    pallas_call x1, Pallas kernels: 50.6 us -> 47.1 us  [on_device(): pl.pallas_call(functools.partial(kernel, planes, rows_y, gz, gy, part, pa...]
where the time goes in v3:
time: 49.5 us; the launch traced here: 49.3 us
  Pallas kernels  47.1 us (95%)
  local copies, waits for them, and re-layouts  2.22 us (4%)
    pallas_call x1, Pallas kernels, on_device(): pl.pallas_call(functools.partial(kernel, planes, rows_y, gz, gy, part, pa...  47.1 us
    unnamed x1, local copies, waits for them, and re-layouts  2.22 us

profile of v3, /device:TPU:0, one launch (start us, length us, event | category | flops | bytes accessed | tf_op | source)
XLA Modules:
  0.0 49.3 jit_solution(4511598653305939093)
XLA Ops:
  0.0 47.1 %shard_map.91 = f32[8,30976]{1,0:T(8,128)} custom-call(f32[8,30976]{1,0:T(8,128)} %density.1, bf16[3,352,128]{2,1,0:T(8,128)(2,1)} %constant.16.clone.refs_0_, bf16[3,352,128]{2,1,0:T(8,128)(2,1)} %constant.17.clone.refs_1_, bf16[3,128,384]{2,1,0:T(8,128)(2,1)} %constant.18.clone.refs_2_, bf16[3,128,384]{2,1,0:T(8,128)(2,1)} %constant.19.clone.refs_3_, ...), custom_call_target="tpu_custom_call" | custom-call | tf_op jit(solution)/shard_map/pallas_call | solution.py:316
  47.1 2.2 %copy.11 = f32[8,30976]{1,0:T(8,128)} copy(f32[8,30976]{1,0:T(8,128)} %shard_map.91) | data formatting | bytes 1982464
